TPU v7x, 32 devices: a 4x4x1 block of a 4x4x8 slice. The times are simulated.
32 devices in a mesh: data: 1 (over z), group: 32 (over y, x, core).
Axes of the slice: x: 4, y: 4, z: 1, core: 2. Of those that a mesh axis runs over, the one named last changes fastest.
The devices are a block of a 4x4x8 slice.
Arguments:
- latents: bfloat16 [4096, 1152], P(('data', 'group'))
- hint_embed: bfloat16 [4096, 1152], P(('data', 'group'))
- in_qkv: bfloat16 [2, 3, 1152, 3456], replicated
- in_proj: bfloat16 [2, 3, 16, 72, 1152], replicated
- in_up: bfloat16 [2, 3, 1152, 4608], replicated
- in_down: bfloat16 [2, 3, 4608, 1152], replicated
- in_norm: bfloat16 [2, 3, 4, 1152], replicated
- out_qkv: bfloat16 [2, 1152, 3456], replicated
- out_proj: bfloat16 [2, 16, 72, 1152], replicated
- out_up: bfloat16 [2, 1152, 4608], replicated
- out_down: bfloat16 [2, 4608, 1152], replicated
- out_norm: bfloat16 [2, 4, 1152], replicated
- zero_proj: bfloat16 [3, 1152, 1152], replicated
- hint_proj: bfloat16 [1152, 1152], replicated
- skip_proj: bfloat16 [2, 2304, 1152], replicated
- final_norm: bfloat16 [2, 1152], replicated
- w_out: bfloat16 [1152, 1152], replicated
Outputs:
- output: bfloat16 [4096, 1152], P(('data', 'group'))
All inputs are finite; a program needn't handle non-finite values.
Results may differ from a plain program's by a relative error of at most 0.02.
Values are sent between devices in bfloat16 or wider.
A program may use at most 768 MiB of HBM per device.

v0:
```python
import jax
import jax.numpy as jnp
from jax import lax
from jax.sharding import PartitionSpec as P

EPS = 1e-6


def mat_f32(left_op, right_op):
    return jnp.dot(left_op, right_op, preferred_element_type=jnp.float32)


def layer_norm(values, norm_gain, norm_shift):
    wide_vals = values.astype(jnp.float32)
    centered = wide_vals - jnp.mean(wide_vals, axis=-1, keepdims=True)
    variance = jnp.mean(centered * centered, axis=-1, keepdims=True)
    normed = centered * lax.rsqrt(variance + EPS)
    return (normed * norm_gain.astype(jnp.float32) + norm_shift.astype(jnp.float32)).astype(jnp.bfloat16)


def gather_half(local_rows, half_size):
    gathered = local_rows
    offset_bit = 1
    while offset_bit < half_size:
        partner_perm = [(dev_id, dev_id ^ offset_bit) for dev_id in range(2 * half_size)]
        gathered = jnp.concatenate([gathered, lax.ppermute(gathered, "group", partner_perm)], axis=0)
        offset_bit = offset_bit * 2
    return gathered


def transformer_block(residual, w_qkv, w_proj, w_up, w_down, norm_rows, half_size):
    tok_count, model_width = residual.shape
    head_count, head_dim = w_proj.shape[0], w_proj.shape[1]
    normed = layer_norm(residual, norm_rows[0], norm_rows[1])
    qkv_all = mat_f32(normed, w_qkv).astype(jnp.bfloat16)
    queries = qkv_all[:, :model_width].reshape(tok_count, head_count, head_dim)
    key_vals = gather_half(qkv_all[:, model_width:], half_size)
    key_heads = key_vals[:, :model_width].reshape(-1, head_count, head_dim)
    val_heads = key_vals[:, model_width:].reshape(-1, head_count, head_dim)
    scores = jnp.einsum("thd,nhd->htn", queries, key_heads, preferred_element_type=jnp.float32) * head_dim ** -0.5
    att_probs = jax.nn.softmax(scores, axis=-1).astype(jnp.bfloat16)
    head_out = jnp.einsum("htn,nhd->thd", att_probs, val_heads, preferred_element_type=jnp.float32).astype(jnp.bfloat16)
    attn_sum = jnp.einsum("thd,hde->te", head_out, w_proj, preferred_element_type=jnp.float32)
    residual = (residual.astype(jnp.float32) + attn_sum).astype(jnp.bfloat16)
    normed = layer_norm(residual, norm_rows[2], norm_rows[3])
    hidden = jax.nn.gelu(mat_f32(normed, w_up), approximate=True).astype(jnp.bfloat16)
    return (residual.astype(jnp.float32) + mat_f32(hidden, w_down)).astype(jnp.bfloat16)


def solution(mesh):
    group_size = mesh.shape["group"]
    half_size = group_size // 2
    swap_perm = [(dev_id, (dev_id + half_size) % group_size) for dev_id in range(group_size)]
    to_base = [(dev_id + half_size, dev_id) for dev_id in range(half_size)]
    to_ctrl = [(dev_id, dev_id + half_size) for dev_id in range(half_size)]

    def device_step(x_own, hint_own, in_qkv, in_proj, in_up, in_down, in_norm, out_qkv, out_proj, out_up, out_down, out_norm, zero_proj, hint_proj, skip_proj, final_norm, w_out):
        layers = skip_proj.shape[0]
        tok_own, model_width = x_own.shape
        branch = lax.axis_index("group") // half_size
        is_base = branch == 0
        x_other = lax.ppermute(x_own, "group", swap_perm)
        hint_recv = lax.ppermute(hint_own, "group", to_ctrl)
        x_local = jnp.where(is_base, jnp.concatenate([x_own, x_other], axis=0), jnp.concatenate([x_other, x_own], axis=0))
        hint_local = jnp.where(is_base, jnp.zeros((2 * tok_own, model_width), jnp.bfloat16), jnp.concatenate([hint_recv, hint_own], axis=0))
        residual = (x_local.astype(jnp.float32) + mat_f32(hint_local, hint_proj)).astype(jnp.bfloat16)
        sum_list = []
        for layer_idx in range(layers + 1):
            residual = transformer_block(residual, in_qkv[branch, layer_idx], in_proj[branch, layer_idx], in_up[branch, layer_idx], in_down[branch, layer_idx], in_norm[branch, layer_idx], half_size)
            ctrl_res = mat_f32(residual, zero_proj[layer_idx]).astype(jnp.bfloat16)
            res_recv = lax.ppermute(ctrl_res, "group", to_base)
            sum_list.append((residual.astype(jnp.float32) + res_recv.astype(jnp.float32)).astype(jnp.bfloat16))
        out_state = sum_list.pop()
        for layer_idx in range(layers):
            skip_val = sum_list[layers - 1 - layer_idx]
            top_part = mat_f32(out_state, skip_proj[layer_idx, :model_width])
            low_part = mat_f32(skip_val, skip_proj[layer_idx, model_width:])
            merged = (top_part + low_part).astype(jnp.bfloat16)
            out_state = transformer_block(merged, out_qkv[layer_idx], out_proj[layer_idx], out_up[layer_idx], out_down[layer_idx], out_norm[layer_idx], half_size)
        normed = layer_norm(out_state, final_norm[0], final_norm[1])
        y_local = mat_f32(normed, w_out).astype(jnp.bfloat16)
        y_recv = lax.ppermute(y_local[tok_own:], "group", to_ctrl)
        return jnp.where(is_base, y_local[:tok_own], y_recv)

    tok_spec = P(("data", "group"), None)
    return jax.shard_map(device_step, mesh=mesh, in_specs=(tok_spec, tok_spec) + (P(),) * 15, out_specs=tok_spec, check_vma=False)
```

profile of v0, /device:TPU:97, one launch (start us, length us, event | category | flops | bytes accessed | tf_op | source)
XLA Modules:
  0.0 2593.7 jit_solution(7656016103612710618)
XLA Ops:
  0.0 4.8 collective-permute-start
  11.6 5.3 collective-permute-done.1
  19.5 6.0 fusion.91
  32.5 51.1 %collective-permute-done.3 = bf16[512,2304]{1,0:T(8,128)(2,1)S(1)} collective-permute-done((bf16[512,2304]{1,0:T(8,128)(2,1)S(1)}, bf16[512,2304]{1,0:T(8,128)(2,1)S(1)}, u32[]{:S(2)}, u32[]{:S(2)}) %collective-permute-start.3) | collective-permute-done | bytes 2359328 | tf_op jit(solution)/shard_map/ppermute | solution.py:26
  87.2 100.7 %collective-permute-done.4 = bf16[1024,2304]{1,0:T(8,128)(2,1)S(1)} collective-permute-done((bf16[1024,2304]{1,0:T(8,128)(2,1)S(1)}, bf16[1024,2304]{1,0:T(8,128)(2,1)S(1)}, u32[]{:S(2)}, u32[]{:S(2)}) %collective-permute-start.4) | collective-permute-done | bytes 4718624 | tf_op jit(solution)/shard_map/ppermute | solution.py:26
  188.0 17.9 pad_maximum_fusion
  214.4 193.7 %collective-permute-done.5 = bf16[2048,2304]{1,0:T(8,128)(2,1)} collective-permute-done((bf16[2048,2304]{1,0:T(8,128)(2,1)}, bf16[2048,2304]{1,0:T(8,128)(2,1)}, u32[]{:S(2)}, u32[]{:S(2)}) %collective-permute-start.5) | collective-permute-done | bytes 9437216 | tf_op jit(solution)/shard_map/ppermute | solution.py:26
  408.2 8.0 constant_dynamic-update-slice_fusion
  416.2 14.6 fusion.586
  430.8 12.9 copy.30
  443.7 12.5 copy.28
  456.2 22.7 fusion.592
  479.0 28.4 %fusion.383 = bf16[256,16,72]{0,2,1:T(8,128)(2,1)S(1)} fusion(bf16[4096,16,72]{0,2,1:T(8,128)(2,1)} %bitcast.356, f32[16,256]{1,0:T(8,128)S(1)} %fusion.592, bf16[256,16,72]{0,2,1:T(8,128)(2,1)S(1)} %bitcast.362, bf16[4096,16,72]{0,2,1:T(8,128)(2,1)} %bitcast.347), kind=kOutput, calls=%fused_computation.251 | convolution fusion | flops 4899250176 | bytes 20070400 | tf_op jit(solution)/shard_map/htn,nhd->thd/dot_general | solution.py:42
  510.6 13.6 convert_reduce_fusion.1
  524.5 6.0 fusion.94
  538.7 51.2 %collective-permute-done.7 = bf16[512,2304]{1,0:T(8,128)(2,1)S(1)} collective-permute-done((bf16[512,2304]{1,0:T(8,128)(2,1)S(1)}, bf16[512,2304]{1,0:T(8,128)(2,1)S(1)}, u32[]{:S(2)}, u32[]{:S(2)}) %collective-permute-start.7) | collective-permute-done | bytes 2359328 | tf_op jit(solution)/shard_map/ppermute | solution.py:26
  593.2 100.8 %collective-permute-done.8 = bf16[1024,2304]{1,0:T(8,128)(2,1)S(1)} collective-permute-done((bf16[1024,2304]{1,0:T(8,128)(2,1)S(1)}, bf16[1024,2304]{1,0:T(8,128)(2,1)S(1)}, u32[]{:S(2)}, u32[]{:S(2)}) %collective-permute-start.8) | collective-permute-done | bytes 4718624 | tf_op jit(solution)/shard_map/ppermute | solution.py:26
  694.0 18.0 pad_maximum_fusion.1
  720.7 193.6 %collective-permute-done.9 = bf16[2048,2304]{1,0:T(8,128)(2,1)} collective-permute-done((bf16[2048,2304]{1,0:T(8,128)(2,1)}, bf16[2048,2304]{1,0:T(8,128)(2,1)}, u32[]{:S(2)}, u32[]{:S(2)}) %collective-permute-start.9) | collective-permute-done | bytes 9437216 | tf_op jit(solution)/shard_map/ppermute | solution.py:26
  914.3 8.0 constant_dynamic-update-slice_fusion.5
  922.3 14.6 fusion.585
  936.9 12.9 copy.33
  949.8 12.5 copy.31
  962.3 22.7 fusion.596
  985.1 28.2 %fusion.388 = bf16[256,16,72]{0,2,1:T(8,128)(2,1)S(1)} fusion(bf16[4096,16,72]{0,2,1:T(8,128)(2,1)} %bitcast.357, f32[16,256]{1,0:T(8,128)S(1)} %fusion.596, bf16[256,16,72]{0,2,1:T(8,128)(2,1)S(1)} %bitcast.364, bf16[4096,16,72]{0,2,1:T(8,128)(2,1)} %bitcast.349), kind=kOutput, calls=%fused_computation.252 | convolution fusion | flops 4899250176 | bytes 20070400 | tf_op jit(solution)/shard_map/htn,nhd->thd/dot_general | solution.py:42
  1016.5 13.6 convert_reduce_fusion
  1030.4 6.0 fusion.97
  1044.8 51.2 %collective-permute-done.11 = bf16[512,2304]{1,0:T(8,128)(2,1)S(1)} collective-permute-done((bf16[512,2304]{1,0:T(8,128)(2,1)S(1)}, bf16[512,2304]{1,0:T(8,128)(2,1)S(1)}, u32[]{:S(2)}, u32[]{:S(2)}) %collective-permute-start.11) | collective-permute-done | bytes 2359328 | tf_op jit(solution)/shard_map/ppermute | solution.py:26
  1099.4 100.8 %collective-permute-done.12 = bf16[1024,2304]{1,0:T(8,128)(2,1)S(1)} collective-permute-done((bf16[1024,2304]{1,0:T(8,128)(2,1)S(1)}, bf16[1024,2304]{1,0:T(8,128)(2,1)S(1)}, u32[]{:S(2)}, u32[]{:S(2)}) %collective-permute-start.12) | collective-permute-done | bytes 4718624 | tf_op jit(solution)/shard_map/ppermute | solution.py:26
  1200.2 18.3 pad_maximum_fusion.2
  1232.0 188.8 %collective-permute-done.13 = bf16[2048,2304]{1,0:T(8,128)(2,1)} collective-permute-done((bf16[2048,2304]{1,0:T(8,128)(2,1)}, bf16[2048,2304]{1,0:T(8,128)(2,1)}, u32[]{:S(2)}, u32[]{:S(2)}) %collective-permute-start.13) | collective-permute-done | bytes 9437216 | tf_op jit(solution)/shard_map/ppermute | solution.py:26
  1420.7 8.0 constant_dynamic-update-slice_fusion.10
  1428.7 14.8 fusion.584
  1443.5 12.9 copy.36
  1456.4 12.5 copy.34
  1468.9 22.7 fusion.600
  1491.7 28.4 %fusion.393 = bf16[256,16,72]{0,2,1:T(8,128)(2,1)S(1)} fusion(bf16[4096,16,72]{0,2,1:T(8,128)(2,1)} %bitcast.358, f32[16,256]{1,0:T(8,128)S(1)} %fusion.600, bf16[256,16,72]{0,2,1:T(8,128)(2,1)S(1)} %bitcast.366, bf16[4096,16,72]{0,2,1:T(8,128)(2,1)} %bitcast.351), kind=kOutput, calls=%fused_computation.253 | convolution fusion | flops 4899250176 | bytes 20070400 | tf_op jit(solution)/shard_map/htn,nhd->thd/dot_general | solution.py:42
  1523.3 13.5 fusion.282
  1545.0 7.5 collective-permute-done.14
  1555.7 6.1 fusion.85
  1563.0 6.8 collective-permute-start.16
  1573.8 51.2 %collective-permute-done.17 = bf16[512,2304]{1,0:T(8,128)(2,1)S(1)} collective-permute-done((bf16[512,2304]{1,0:T(8,128)(2,1)S(1)}, bf16[512,2304]{1,0:T(8,128)(2,1)S(1)}, u32[]{:S(2)}, u32[]{:S(2)}) %collective-permute-start.17) | collective-permute-done | bytes 2359328 | tf_op jit(solution)/shard_map/ppermute | solution.py:26
  1628.4 100.8 %collective-permute-done.18 = bf16[1024,2304]{1,0:T(8,128)(2,1)S(1)} collective-permute-done((bf16[1024,2304]{1,0:T(8,128)(2,1)S(1)}, bf16[1024,2304]{1,0:T(8,128)(2,1)S(1)}, u32[]{:S(2)}, u32[]{:S(2)}) %collective-permute-start.18) | collective-permute-done | bytes 4718624 | tf_op jit(solution)/shard_map/ppermute | solution.py:26
  1729.1 17.9 pad_maximum_fusion.3
  1760.6 188.7 %collective-permute-done.19 = bf16[2048,2304]{1,0:T(8,128)(2,1)} collective-permute-done((bf16[2048,2304]{1,0:T(8,128)(2,1)}, bf16[2048,2304]{1,0:T(8,128)(2,1)}, u32[]{:S(2)}, u32[]{:S(2)}) %collective-permute-start.19) | collective-permute-done | bytes 9437216 | tf_op jit(solution)/shard_map/ppermute | solution.py:26
  1949.3 8.0 constant_dynamic-update-slice_fusion.15
  1957.3 14.6 fusion.583
  1971.9 12.9 copy.39
  1984.8 12.5 copy.37
  1997.3 22.7 fusion.603
  2020.1 28.5 %fusion.398 = bf16[256,16,72]{0,2,1:T(8,128)(2,1)S(1)} fusion(bf16[4096,16,72]{0,2,1:T(8,128)(2,1)} %bitcast.359, f32[16,256]{1,0:T(8,128)S(1)} %fusion.603, bf16[256,16,72]{0,2,1:T(8,128)(2,1)S(1)} %bitcast.368, bf16[4096,16,72]{0,2,1:T(8,128)(2,1)} %bitcast.353), kind=kOutput, calls=%fused_computation.254 | convolution fusion | flops 4899250176 | bytes 20070400 | tf_op jit(solution)/shard_map/htn,nhd->thd/dot_general | solution.py:42
  2051.7 13.5 fusion.321
  2071.5 6.1 fusion.88
  2085.7 51.2 %collective-permute-done.22 = bf16[512,2304]{1,0:T(8,128)(2,1)S(1)} collective-permute-done((bf16[512,2304]{1,0:T(8,128)(2,1)S(1)}, bf16[512,2304]{1,0:T(8,128)(2,1)S(1)}, u32[]{:S(2)}, u32[]{:S(2)}) %collective-permute-start.22) | collective-permute-done | bytes 2359328 | tf_op jit(solution)/shard_map/ppermute | solution.py:26
  2140.3 100.8 %collective-permute-done.23 = bf16[1024,2304]{1,0:T(8,128)(2,1)S(1)} collective-permute-done((bf16[1024,2304]{1,0:T(8,128)(2,1)S(1)}, bf16[1024,2304]{1,0:T(8,128)(2,1)S(1)}, u32[]{:S(2)}, u32[]{:S(2)}) %collective-permute-start.23) | collective-permute-done | bytes 4718624 | tf_op jit(solution)/shard_map/ppermute | solution.py:26
  2241.1 18.0 pad_maximum_fusion.4
  2268.3 193.1 %collective-permute-done.24 = bf16[2048,2304]{1,0:T(8,128)(2,1)} collective-permute-done((bf16[2048,2304]{1,0:T(8,128)(2,1)}, bf16[2048,2304]{1,0:T(8,128)(2,1)}, u32[]{:S(2)}, u32[]{:S(2)}) %collective-permute-start.24) | collective-permute-done | bytes 9437216 | tf_op jit(solution)/shard_map/ppermute | solution.py:26
  2461.4 8.0 constant_dynamic-update-slice_fusion.20
  2469.4 14.6 fusion.582
  2484.0 12.9 copy.42
  2496.9 12.5 copy.40
  2509.4 22.7 fusion.606
  2532.2 28.6 %fusion.403 = bf16[256,16,72]{0,2,1:T(8,128)(2,1)S(1)} fusion(bf16[4096,16,72]{0,2,1:T(8,128)(2,1)} %bitcast.360, f32[16,256]{1,0:T(8,128)S(1)} %fusion.606, bf16[256,16,72]{0,2,1:T(8,128)(2,1)S(1)} %bitcast.370, bf16[4096,16,72]{0,2,1:T(8,128)(2,1)} %bitcast.355), kind=kOutput, calls=%fused_computation.255 | convolution fusion | flops 4899250176 | bytes 20070400 | tf_op jit(solution)/shard_map/htn,nhd->thd/dot_general | solution.py:42
  2565.0 15.2 fusion.608
  (240 shorter events, 164.8 us)
Async XLA Ops:
  0.0 16.9 copy-start
  0.0 11.6 collective-permute-start
  4.8 12.1 collective-permute-start.1
  19.2 6.3 copy-start.30
  26.7 4.2 collective-permute-start.2
  30.9 157.1 %copy-start.5 = (bf16[256,2304]{1,0:T(8,128)(2,1)}, bf16[256,2304]{1,0:T(8,128)(2,1)S(1)}, u32[]{:S(2)}) copy-start(bf16[256,2304]{1,0:T(8,128)(2,1)S(1)} %collective-permute-done.2) | copy-start | bytes 3538948
  31.0 52.5 %collective-permute-start.3 = (bf16[512,2304]{1,0:T(8,128)(2,1)S(1)}, bf16[512,2304]{1,0:T(8,128)(2,1)S(1)}, u32[]{:S(2)}, u32[]{:S(2)}) collective-permute-start(bf16[512,2304]{1,0:T(8,128)(2,1)S(1)} %pad_maximum_fusion.10), channel_id=1, source_target_pairs={{0,2},{1,3},{2,0},{3,1},{4,6},{5,7},{6,4},{7,5},{8,10},{9,11},{10,... | collective-permute-start | bytes 7077896 | tf_op jit(solution)/shard_map/ppermute | solution.py:26
  84.1 103.8 %collective-permute-start.4 = (bf16[1024,2304]{1,0:T(8,128)(2,1)S(1)}, bf16[1024,2304]{1,0:T(8,128)(2,1)S(1)}, u32[]{:S(2)}, u32[]{:S(2)}) collective-permute-start(bf16[1024,2304]{1,0:T(8,128)(2,1)S(1)} %pad_maximum_fusion.5), channel_id=1, source_target_pairs={{0,4},{1,5},{2,6},{3,7},{4,0},{5,1},{6,2},{7,3},{8,12},{9,13},{10,... | collective-permute-start | bytes 14155784 | tf_op jit(solution)/shard_map/ppermute | solution.py:26
  188.0 17.9 copy-start.13
  205.8 202.3 %collective-permute-start.5 = (bf16[2048,2304]{1,0:T(8,128)(2,1)}, bf16[2048,2304]{1,0:T(8,128)(2,1)}, u32[]{:S(2)}, u32[]{:S(2)}) collective-permute-start(bf16[2048,2304]{1,0:T(8,128)(2,1)} %pad_maximum_fusion), channel_id=1, source_target_pairs={{0,8},{1,9},{2,10},{3,11},{4,12},{5,13},{6,14},{7,15},{8,0},{9,1},... | collective-permute-start | bytes 28311560 | tf_op jit(solution)/shard_map/ppermute | solution.py:26
  443.7 12.5 copy-start.32
  478.9 28.4 %copy-start.31 = (bf16[256,1152]{1,0:T(8,128)(2,1)S(1)}, bf16[256,1152]{1,0:T(8,128)(2,1)}, u32[]{:S(2)}) copy-start(bf16[256,1152]{1,0:T(8,128)(2,1)} %copy-done.30) | copy-start | bytes 1769476
  510.6 13.9 copy-start.49
  510.6 13.9 copy-start.50
  524.1 6.4 copy-start.23
  531.7 5.5 collective-permute-start.6
  537.2 156.8 %copy-start.6 = (bf16[256,2304]{1,0:T(8,128)(2,1)}, bf16[256,2304]{1,0:T(8,128)(2,1)S(1)}, u32[]{:S(2)}) copy-start(bf16[256,2304]{1,0:T(8,128)(2,1)S(1)} %collective-permute-done.6) | copy-start | bytes 3538948
  537.3 52.5 %collective-permute-start.7 = (bf16[512,2304]{1,0:T(8,128)(2,1)S(1)}, bf16[512,2304]{1,0:T(8,128)(2,1)S(1)}, u32[]{:S(2)}, u32[]{:S(2)}) collective-permute-start(bf16[512,2304]{1,0:T(8,128)(2,1)S(1)} %pad_maximum_fusion.11), channel_id=1, source_target_pairs={{0,2},{1,3},{2,0},{3,1},{4,6},{5,7},{6,4},{7,5},{8,10},{9,11},{10,... | collective-permute-start | bytes 7077896 | tf_op jit(solution)/shard_map/ppermute | solution.py:26
  590.2 103.7 %collective-permute-start.8 = (bf16[1024,2304]{1,0:T(8,128)(2,1)S(1)}, bf16[1024,2304]{1,0:T(8,128)(2,1)S(1)}, u32[]{:S(2)}, u32[]{:S(2)}) collective-permute-start(bf16[1024,2304]{1,0:T(8,128)(2,1)S(1)} %pad_maximum_fusion.6), channel_id=1, source_target_pairs={{0,4},{1,5},{2,6},{3,7},{4,0},{5,1},{6,2},{7,3},{8,12},{9,13},{10,... | collective-permute-start | bytes 14155784 | tf_op jit(solution)/shard_map/ppermute | solution.py:26
  694.0 18.0 copy-start.15
  712.0 202.3 %collective-permute-start.9 = (bf16[2048,2304]{1,0:T(8,128)(2,1)}, bf16[2048,2304]{1,0:T(8,128)(2,1)}, u32[]{:S(2)}, u32[]{:S(2)}) collective-permute-start(bf16[2048,2304]{1,0:T(8,128)(2,1)} %pad_maximum_fusion.1), channel_id=1, source_target_pairs={{0,8},{1,9},{2,10},{3,11},{4,12},{5,13},{6,14},{7,15},{8,0},{9,1},... | collective-permute-start | bytes 28311560 | tf_op jit(solution)/shard_map/ppermute | solution.py:26
  949.8 12.5 copy-start.33
  985.1 28.2 %copy-start.24 = (bf16[256,1152]{1,0:T(8,128)(2,1)S(1)}, bf16[256,1152]{1,0:T(8,128)(2,1)}, u32[]{:S(2)}) copy-start(bf16[256,1152]{1,0:T(8,128)(2,1)} %copy-done.23) | copy-start | bytes 1769476
  1016.5 13.9 copy-start.43
  1016.5 13.9 copy-start.44
  1030.1 6.4 copy-start.27
  1036.5 182.9 %copy-start.22 = (bf16[256,3456]{1,0:T(8,128)(2,1)}, bf16[256,3456]{1,0:T(8,128)(2,1)S(1)}, u32[]{:S(2)}) copy-start(bf16[256,3456]{1,0:T(8,128)(2,1)S(1)} %fusion.97) | copy-start | bytes 5308420
  1037.8 5.5 collective-permute-start.10
  1043.3 156.8 %copy-start.2 = (bf16[256,2304]{1,0:T(8,128)(2,1)}, bf16[256,2304]{1,0:T(8,128)(2,1)S(1)}, u32[]{:S(2)}) copy-start(bf16[256,2304]{1,0:T(8,128)(2,1)S(1)} %collective-permute-done.10) | copy-start | bytes 3538948
  1043.5 52.5 %collective-permute-start.11 = (bf16[512,2304]{1,0:T(8,128)(2,1)S(1)}, bf16[512,2304]{1,0:T(8,128)(2,1)S(1)}, u32[]{:S(2)}, u32[]{:S(2)}) collective-permute-start(bf16[512,2304]{1,0:T(8,128)(2,1)S(1)} %pad_maximum_fusion.12), channel_id=1, source_target_pairs={{0,2},{1,3},{2,0},{3,1},{4,6},{5,7},{6,4},{7,5},{8,10},{9,11},{10,... | collective-permute-start | bytes 7077896 | tf_op jit(solution)/shard_map/ppermute | solution.py:26
  1096.4 123.0 %copy-start.28 = (bf16[256,1152]{1,0:T(8,128)(2,1)S(1)}, bf16[256,1152]{1,0:T(8,128)(2,1)}, u32[]{:S(2)}) copy-start(bf16[256,1152]{1,0:T(8,128)(2,1)} %copy-done.27) | copy-start | bytes 1769476
  1096.4 103.7 %collective-permute-start.12 = (bf16[1024,2304]{1,0:T(8,128)(2,1)S(1)}, bf16[1024,2304]{1,0:T(8,128)(2,1)S(1)}, u32[]{:S(2)}, u32[]{:S(2)}) collective-permute-start(bf16[1024,2304]{1,0:T(8,128)(2,1)S(1)} %pad_maximum_fusion.7), channel_id=1, source_target_pairs={{0,4},{1,5},{2,6},{3,7},{4,0},{5,1},{6,2},{7,3},{8,12},{9,13},{10,... | collective-permute-start | bytes 14155784 | tf_op jit(solution)/shard_map/ppermute | solution.py:26
  1200.2 18.3 copy-start.7
  1218.4 202.3 %collective-permute-start.13 = (bf16[2048,2304]{1,0:T(8,128)(2,1)}, bf16[2048,2304]{1,0:T(8,128)(2,1)}, u32[]{:S(2)}, u32[]{:S(2)}) collective-permute-start(bf16[2048,2304]{1,0:T(8,128)(2,1)} %pad_maximum_fusion.2), channel_id=1, source_target_pairs={{0,8},{1,9},{2,10},{3,11},{4,12},{5,13},{6,14},{7,15},{8,0},{9,1},... | collective-permute-start | bytes 28311560 | tf_op jit(solution)/shard_map/ppermute | solution.py:26
  1219.4 5.0 slice-start
  1223.0 319.1 %collective-permute-start.15 = (bf16[256,1152]{1,0:T(8,128)(2,1)}, bf16[256,1152]{1,0:T(8,128)(2,1)}, u32[]{:S(2)}, u32[]{:S(2)}) collective-permute-start(bf16[256,1152]{1,0:T(8,128)(2,1)} %fusion.264), channel_id=1, source_target_pairs={{16,0},{17,1},{18,2},{19,3},{20,4},{21,5},{22,6},{23,7},{24,8},{25... | collective-permute-start | bytes 1769480 | tf_op jit(solution)/shard_map/ppermute | solution.py:71
  1456.4 12.5 copy-start.34
  1491.7 28.5 %copy-start.29 = (bf16[256,1152]{1,0:T(8,128)(2,1)S(1)}, bf16[256,1152]{1,0:T(8,128)(2,1)}, u32[]{:S(2)}) copy-start(bf16[256,1152]{1,0:T(8,128)(2,1)} %copy-done.27) | copy-start | bytes 1769476
  1539.6 13.0 collective-permute-start.14
  1555.4 6.4 copy-start.17
  1563.0 9.3 collective-permute-start.16
  1572.3 156.8 %copy-start.3 = (bf16[256,2304]{1,0:T(8,128)(2,1)}, bf16[256,2304]{1,0:T(8,128)(2,1)S(1)}, u32[]{:S(2)}) copy-start(bf16[256,2304]{1,0:T(8,128)(2,1)S(1)} %collective-permute-done.16) | copy-start | bytes 3538948
  1572.4 52.5 %collective-permute-start.17 = (bf16[512,2304]{1,0:T(8,128)(2,1)S(1)}, bf16[512,2304]{1,0:T(8,128)(2,1)S(1)}, u32[]{:S(2)}, u32[]{:S(2)}) collective-permute-start(bf16[512,2304]{1,0:T(8,128)(2,1)S(1)} %pad_maximum_fusion.13), channel_id=1, source_target_pairs={{0,2},{1,3},{2,0},{3,1},{4,6},{5,7},{6,4},{7,5},{8,10},{9,11},{10,... | collective-permute-start | bytes 7077896 | tf_op jit(solution)/shard_map/ppermute | solution.py:26
  1625.4 122.5 %copy-start.25 = (bf16[256,1152]{1,0:T(8,128)(2,1)S(1)}, bf16[256,1152]{1,0:T(8,128)(2,1)}, u32[]{:S(2)}) copy-start(bf16[256,1152]{1,0:T(8,128)(2,1)} %copy-done.23) | copy-start | bytes 1769476
  1625.4 103.7 %collective-permute-start.18 = (bf16[1024,2304]{1,0:T(8,128)(2,1)S(1)}, bf16[1024,2304]{1,0:T(8,128)(2,1)S(1)}, u32[]{:S(2)}, u32[]{:S(2)}) collective-permute-start(bf16[1024,2304]{1,0:T(8,128)(2,1)S(1)} %pad_maximum_fusion.8), channel_id=1, source_target_pairs={{0,4},{1,5},{2,6},{3,7},{4,0},{5,1},{6,2},{7,3},{8,12},{9,13},{10,... | collective-permute-start | bytes 14155784 | tf_op jit(solution)/shard_map/ppermute | solution.py:26
  1729.1 17.9 copy-start.9
  1747.0 202.3 %collective-permute-start.19 = (bf16[2048,2304]{1,0:T(8,128)(2,1)}, bf16[2048,2304]{1,0:T(8,128)(2,1)}, u32[]{:S(2)}, u32[]{:S(2)}) collective-permute-start(bf16[2048,2304]{1,0:T(8,128)(2,1)} %pad_maximum_fusion.3), channel_id=1, source_target_pairs={{0,8},{1,9},{2,10},{3,11},{4,12},{5,13},{6,14},{7,15},{8,0},{9,1},... | collective-permute-start | bytes 28311560 | tf_op jit(solution)/shard_map/ppermute | solution.py:26
  1751.4 316.7 %collective-permute-start.20 = (bf16[256,1152]{1,0:T(8,128)(2,1)}, bf16[256,1152]{1,0:T(8,128)(2,1)}, u32[]{:S(2)}, u32[]{:S(2)}) collective-permute-start(bf16[256,1152]{1,0:T(8,128)(2,1)} %fusion.267), channel_id=1, source_target_pairs={{16,0},{17,1},{18,2},{19,3},{20,4},{21,5},{22,6},{23,7},{24,8},{25... | collective-permute-start | bytes 1769480 | tf_op jit(solution)/shard_map/ppermute | solution.py:71
  1984.8 12.5 copy-start.35
  2020.0 28.5 %copy-start.18 = (f32[256,1152]{1,0:T(8,128)S(1)}, f32[256,1152]{1,0:T(8,128)}, u32[]{:S(2)}) copy-start(f32[256,1152]{1,0:T(8,128)} %copy-done.17) | copy-start | bytes 3538948
  2071.2 6.4 copy-start.19
  2078.7 5.5 collective-permute-start.21
  2084.2 156.8 %copy-start.4 = (bf16[256,2304]{1,0:T(8,128)(2,1)}, bf16[256,2304]{1,0:T(8,128)(2,1)S(1)}, u32[]{:S(2)}) copy-start(bf16[256,2304]{1,0:T(8,128)(2,1)S(1)} %collective-permute-done.21) | copy-start | bytes 3538948
  2084.4 52.5 %collective-permute-start.22 = (bf16[512,2304]{1,0:T(8,128)(2,1)S(1)}, bf16[512,2304]{1,0:T(8,128)(2,1)S(1)}, u32[]{:S(2)}, u32[]{:S(2)}) collective-permute-start(bf16[512,2304]{1,0:T(8,128)(2,1)S(1)} %pad_maximum_fusion.14), channel_id=1, source_target_pairs={{0,2},{1,3},{2,0},{3,1},{4,6},{5,7},{6,4},{7,5},{8,10},{9,11},{10,... | collective-permute-start | bytes 7077896 | tf_op jit(solution)/shard_map/ppermute | solution.py:26
  2137.3 122.7 %copy-start.38 = (bf16[2,1152]{1,0:T(2,128)(2,1)S(1)}, bf16[2,1152]{1,0:T(2,128)(2,1)}, u32[]{:S(2)}) copy-start(bf16[2,1152]{1,0:T(2,128)(2,1)} %param.32) | copy-start | bytes 13828
  2137.3 103.7 %collective-permute-start.23 = (bf16[1024,2304]{1,0:T(8,128)(2,1)S(1)}, bf16[1024,2304]{1,0:T(8,128)(2,1)S(1)}, u32[]{:S(2)}, u32[]{:S(2)}) collective-permute-start(bf16[1024,2304]{1,0:T(8,128)(2,1)S(1)} %pad_maximum_fusion.9), channel_id=1, source_target_pairs={{0,4},{1,5},{2,6},{3,7},{4,0},{5,1},{6,2},{7,3},{8,12},{9,13},{10,... | collective-permute-start | bytes 14155784 | tf_op jit(solution)/shard_map/ppermute | solution.py:26
  2241.1 18.0 copy-start.11
  2259.1 202.3 %collective-permute-start.24 = (bf16[2048,2304]{1,0:T(8,128)(2,1)}, bf16[2048,2304]{1,0:T(8,128)(2,1)}, u32[]{:S(2)}, u32[]{:S(2)}) collective-permute-start(bf16[2048,2304]{1,0:T(8,128)(2,1)} %pad_maximum_fusion.4), channel_id=1, source_target_pairs={{0,8},{1,9},{2,10},{3,11},{4,12},{5,13},{6,14},{7,15},{8,0},{9,1},... | collective-permute-start | bytes 28311560 | tf_op jit(solution)/shard_map/ppermute | solution.py:26
  2496.9 12.5 copy-start.36
  2532.2 28.6 %copy-start.20 = (f32[256,1152]{1,0:T(8,128)S(1)}, f32[256,1152]{1,0:T(8,128)}, u32[]{:S(2)}) copy-start(f32[256,1152]{1,0:T(8,128)} %copy-done.19) | copy-start | bytes 3538948
  2565.0 16.8 copy-start.55
  2565.0 16.8 copy-start.56
  2565.0 28.4 %copy-start.1 = (bf16[1152,1152]{1,0:T(8,128)(2,1)S(1)}, bf16[1152,1152]{1,0:T(8,128)(2,1)}, u32[]{:S(2)}) copy-start(bf16[1152,1152]{1,0:T(8,128)(2,1)} %param.30) | copy-start | bytes 7962628
  2585.1 7.6 collective-permute-start.25
  (20 other events, 69.7 us)
where the time goes:
time: 2600 us; the launch traced here: 2590 us
  waiting for transfers between devices  1750 us (67%)
  matrix products  397 us (15%)
  local copies, waits for them, and re-layouts  286 us (11%)
  other arithmetic  101 us (4%)
  starting transfers between devices  59.5 us (2%)
    ppermute x20, waiting for transfers between devices, gather_half(): lax.ppermute(gathered, 'group', partner_perm)  1730 us
    dot_general x5, matrix products, transformer_block(): jnp.einsum('htn,nhd->thd', att_probs, val_heads, preferred_element_type=j...  142 us
    slice x10, local copies, waits for them, and re-layouts, transformer_block(): key_heads = key_vals[:, :model_width].reshape(-1, head_count, head_dim)  138 us
    dot_general x19, matrix products, mat_f32(): return jnp.dot(left_op, right_op, preferred_element_type=jnp.float32)  127 us
    sub x5, matrix products, transformer_block(): att_probs = jax.nn.softmax(scores, axis=-1).astype(jnp.bfloat16)  114 us
    concatenate x15, other arithmetic, gather_half(): jnp.concatenate([gathered, lax.ppermute(gathered, 'group', partner_perm)]...  92.9 us
    slice x5, local copies, waits for them, and re-layouts, transformer_block(): val_heads = key_vals[:, model_width:].reshape(-1, head_count, head_dim)  62.6 us
  transfers between devices with their start and end apart: 26, of which 24 were waited for; matrix products, arithmetic and copies ran while one was open for 11% of the time, Pallas kernels for 0%

commit v1 on v0

v1 whole, which is shorter than its diff:
```python
import functools
import jax
import jax.numpy as jnp
from jax import lax
from jax.experimental import pallas as pl
from jax.experimental.pallas import tpu as pltpu
from jax.sharding import PartitionSpec as P

EPS = 1e-6
LOG2E = 1.4426950408889634
F32 = jnp.float32
BF16 = jnp.bfloat16
VMEM_LIMIT = 60 * 1024 * 1024


def mat_f32(left_op, right_op):
    return jnp.dot(left_op, right_op, preferred_element_type=F32)


def layer_norm(values, norm_gain, norm_shift):
    wide_vals = values.astype(F32)
    centered = wide_vals - jnp.mean(wide_vals, axis=-1, keepdims=True)
    variance = jnp.mean(centered * centered, axis=-1, keepdims=True)
    normed = centered * lax.rsqrt(variance + EPS)
    return (normed * norm_gain.astype(F32) + norm_shift.astype(F32)).astype(BF16)


def qkv_kernel(br_ref, u_ref, norm_ref, w_ref, out_ref, t_ref, *, heads, head_dim):
    @pl.when(pl.program_id(0) == 0)
    def _():
        t_ref[...] = layer_norm(u_ref[...], norm_ref[0, 0, 0:1, :], norm_ref[0, 0, 1:2, :])

    prod = mat_f32(t_ref[...], w_ref[0, 0]).T
    tokens = prod.shape[1]
    out_ref[...] = prod.reshape(heads, 1, head_dim, tokens).astype(BF16)


def qkv_call(branch, layer, u, norm, w_qkv, heads):
    tokens, width = u.shape
    head_dim = width // heads
    grid_spec = pltpu.PrefetchScalarGridSpec(
        num_scalar_prefetch=1,
        grid=(3,),
        in_specs=[
            pl.BlockSpec((tokens, width), lambda n, br: (0, 0)),
            pl.BlockSpec((1, 1, 4, width), lambda n, br: (br[0], layer, 0, 0)),
            pl.BlockSpec((1, 1, width, width), lambda n, br: (br[0], layer, 0, n)),
        ],
        out_specs=pl.BlockSpec((heads, 1, head_dim, tokens), lambda n, br: (0, n, 0, 0)),
        scratch_shapes=[pltpu.VMEM((tokens, width), BF16)],
    )
    return pl.pallas_call(
        functools.partial(qkv_kernel, heads=heads, head_dim=head_dim),
        grid_spec=grid_spec,
        out_shape=jax.ShapeDtypeStruct((heads, 3, head_dim, tokens), BF16),
        compiler_params=pltpu.CompilerParams(vmem_limit_bytes=VMEM_LIMIT, dimension_semantics=("arbitrary",)),
        cost_estimate=pl.CostEstimate(flops=6 * tokens * width * width, bytes_accessed=6 * width * width, transcendentals=0),
        name="ln_qkv",
    )(branch, u, norm, w_qkv)


def post_kernel(br_ref, at_ref, u_ref, norm_ref, wo_ref, w1_ref, w2_ref, out_ref, res_ref, t_ref, acc_ref):
    step = pl.program_id(0)

    @pl.when(step == 0)
    def _():
        att = at_ref[...].T
        res = (u_ref[...].astype(F32) + mat_f32(att, wo_ref[0, 0])).astype(BF16)
        res_ref[...] = res
        t_ref[...] = layer_norm(res, norm_ref[0, 0, 2:3, :], norm_ref[0, 0, 3:4, :])

    hidden = jax.nn.gelu(mat_f32(t_ref[...], w1_ref[0, 0]), approximate=True).astype(BF16)
    part = mat_f32(hidden, w2_ref[0, 0])

    @pl.when(step == 0)
    def _():
        acc_ref[...] = part

    @pl.when(step > 0)
    def _():
        acc_ref[...] += part

    @pl.when(step == pl.num_programs(0) - 1)
    def _():
        out_ref[...] = (res_ref[...].astype(F32) + acc_ref[...]).astype(BF16)


def post_call(branch, layer, att_t, u, norm, w_proj, w_up, w_down):
    tokens, width = u.shape
    hidden = w_up.shape[-1]
    tile = hidden // 6
    grid_spec = pltpu.PrefetchScalarGridSpec(
        num_scalar_prefetch=1,
        grid=(6,),
        in_specs=[
            pl.BlockSpec((width, tokens), lambda n, br: (0, 0)),
            pl.BlockSpec((tokens, width), lambda n, br: (0, 0)),
            pl.BlockSpec((1, 1, 4, width), lambda n, br: (br[0], layer, 0, 0)),
            pl.BlockSpec((1, 1, width, width), lambda n, br: (br[0], layer, 0, 0)),
            pl.BlockSpec((1, 1, width, tile), lambda n, br: (br[0], layer, 0, n)),
            pl.BlockSpec((1, 1, tile, width), lambda n, br: (br[0], layer, n, 0)),
        ],
        out_specs=pl.BlockSpec((tokens, width), lambda n, br: (0, 0)),
        scratch_shapes=[
            pltpu.VMEM((tokens, width), BF16),
            pltpu.VMEM((tokens, width), BF16),
            pltpu.VMEM((tokens, width), F32),
        ],
    )
    return pl.pallas_call(
        post_kernel,
        grid_spec=grid_spec,
        out_shape=jax.ShapeDtypeStruct((tokens, width), BF16),
        compiler_params=pltpu.CompilerParams(vmem_limit_bytes=VMEM_LIMIT, dimension_semantics=("arbitrary",)),
        cost_estimate=pl.CostEstimate(
            flops=2 * tokens * width * (width + 2 * hidden), bytes_accessed=2 * width * (width + 2 * hidden), transcendentals=tokens * hidden
        ),
        name="proj_mlp",
    )(branch, att_t, u, norm, w_proj, w_up, w_down)


def attn_kernel(q_ref, kv_ref, out_ref, q2_ref, k2_ref, v_ref, s_ref, *, scale, chunk, q_tile):
    q_src, head_dim, span = q_ref.shape
    srcs = kv_ref.shape[0]
    keys = srcs * span
    per_q = q_tile // span
    q_tiles = q_src // per_q
    chunks = keys // chunk
    per_chunk = chunk // span
    v_rows = v_ref.shape[1]
    ones_row = (lax.broadcasted_iota(jnp.int32, (v_rows - head_dim, span), 0) == 0).astype(F32)

    def fill_kv(src, carry):
        key_t = kv_ref[src, 0].astype(F32)
        two_keys = jnp.concatenate([key_t, key_t], axis=0)
        k2_ref[pl.ds(pl.multiple_of(src * span, span), span), :] = two_keys.T.astype(BF16)
        val_t = jnp.concatenate([kv_ref[src, 1].astype(F32), ones_row], axis=0).astype(BF16)
        lane = pl.multiple_of(lax.rem(src, per_chunk) * span, span)
        v_ref[src // per_chunk, :, pl.ds(lane, span)] = val_t
        return carry

    lax.fori_loop(0, srcs, fill_kv, 0)

    def fill_q(src, carry):
        wide = q_ref[src].astype(F32) * (scale * LOG2E)
        high = wide.astype(BF16)
        low = (wide - high.astype(F32)).astype(F32)
        both = jnp.concatenate([high.astype(F32), low], axis=0).astype(BF16)
        lane = pl.multiple_of(lax.rem(src, per_q) * span, span)
        q2_ref[src // per_q, :, pl.ds(lane, span)] = both
        return carry

    lax.fori_loop(0, q_src, fill_q, 0)

    def score_chunk(tile, slot, idx, peak):
        part = mat_f32(k2_ref[idx * chunk:(idx + 1) * chunk, :], q2_ref[tile])
        s_ref[slot, idx * chunk:(idx + 1) * chunk, :] = part
        return jnp.maximum(peak, jnp.max(part.reshape(chunk // 8, 8, q_tile), axis=0))

    low_peak = jnp.full((8, q_tile), -jnp.inf, F32)
    peak = low_peak
    for idx in range(chunks):
        peak = score_chunk(0, 0, idx, peak)

    def one_tile(tile, peak):
        slot = lax.rem(tile, 2)
        nxt = jnp.minimum(tile + 1, q_tiles - 1)
        top = jnp.max(peak, axis=0, keepdims=True)
        acc = jnp.zeros((v_rows, q_tile), F32)
        new_peak = low_peak
        for idx in range(chunks):
            new_peak = score_chunk(nxt, 1 - slot, idx, new_peak)
            probs = jnp.exp2(s_ref[slot, idx * chunk:(idx + 1) * chunk, :] - top).astype(BF16)
            acc = acc + mat_f32(v_ref[idx], probs)
        normed = (acc[:head_dim] / acc[head_dim:head_dim + 1]).astype(BF16)
        for sub in range(per_q):
            out_ref[tile * per_q + sub] = normed[:, sub * span:(sub + 1) * span]
        return new_peak

    lax.fori_loop(0, q_tiles, one_tile, peak)


def attn_call(q_t, kv_t, chunk=512, q_tile=256):
    q_src, head_dim, span = q_t.shape
    srcs = kv_t.shape[0]
    keys = srcs * span
    v_rows = head_dim + 8
    return pl.pallas_call(
        functools.partial(attn_kernel, scale=head_dim ** -0.5, chunk=chunk, q_tile=q_tile),
        in_specs=[pl.BlockSpec(memory_space=pltpu.VMEM)] * 2,
        out_specs=pl.BlockSpec(memory_space=pltpu.VMEM),
        out_shape=jax.ShapeDtypeStruct((q_src, head_dim, span), BF16),
        scratch_shapes=[
            pltpu.VMEM((q_src * span // q_tile, 2 * head_dim, q_tile), BF16),
            pltpu.VMEM((keys, 2 * head_dim), BF16),
            pltpu.VMEM((keys // chunk, v_rows, chunk), BF16),
            pltpu.VMEM((2, keys, q_tile), F32),
        ],
        compiler_params=pltpu.CompilerParams(vmem_limit_bytes=VMEM_LIMIT),
        cost_estimate=pl.CostEstimate(
            flops=4 * q_src * span * keys * head_dim, bytes_accessed=4 * keys * head_dim * 4, transcendentals=q_src * span * keys
        ),
        name="attention",
    )(q_t, kv_t)


def barrier_all(peers):
    sem = pltpu.get_barrier_semaphore()
    for peer in peers:
        pl.semaphore_signal(sem, inc=1, device_id={"group": peer}, device_id_type=pl.DeviceIdType.MESH)
    pl.semaphore_wait(sem, len(peers))


def plane_exchange_kernel(x_ref, out_ref, send_sem, recv_sem, own_sem):
    chips = x_ref.shape[0]
    me = lax.axis_index("group")
    chip, core = me // 2, lax.rem(me, 2)
    others = [lax.rem(chip + off, chips) for off in range(1, chips)]
    barrier_all([2 * other + core for other in others])
    own = pltpu.make_async_copy(x_ref.at[chip], out_ref.at[chip], own_sem)
    own.start()
    copies = []
    for off, other in enumerate(others):
        copy = pltpu.make_async_remote_copy(
            src_ref=x_ref.at[other],
            dst_ref=out_ref.at[chip],
            send_sem=send_sem.at[off],
            recv_sem=recv_sem.at[off],
            device_id={"group": 2 * other + core},
            device_id_type=pl.DeviceIdType.MESH,
        )
        copy.start()
        copies.append(copy)
    own.wait()
    for copy in copies:
        copy.wait()


def plane_exchange(x, collective_id):
    chips = x.shape[0]
    return pl.pallas_call(
        plane_exchange_kernel,
        in_specs=[pl.BlockSpec(memory_space=pltpu.VMEM)],
        out_specs=pl.BlockSpec(memory_space=pltpu.VMEM),
        out_shape=jax.ShapeDtypeStruct(x.shape, x.dtype),
        scratch_shapes=[pltpu.SemaphoreType.DMA((chips - 1,)), pltpu.SemaphoreType.DMA((chips - 1,)), pltpu.SemaphoreType.DMA],
        compiler_params=pltpu.CompilerParams(collective_id=collective_id, has_side_effects=True, vmem_limit_bytes=VMEM_LIMIT),
        name="plane_exchange",
    )(x)


def spread_kernel(q_ref, kv_ref, q_out, kv_out, send_sem, recv_sem, own_sem):
    chips = q_ref.shape[0]
    group = 2 * chips
    me = lax.axis_index("group")
    chip, core = me // 2, lax.rem(me, 2)
    barrier_all([lax.rem(me + off, group) for off in range(1, group)])
    own = [
        pltpu.make_async_copy(q_ref.at[chip], q_out.at[chip], own_sem.at[0]),
        pltpu.make_async_copy(kv_ref.at[chip], kv_out.at[me], own_sem.at[1]),
    ]
    for copy in own:
        copy.start()
    copies = []
    for off in range(1, group):
        peer = lax.rem(me + off, group)
        copies.append(pltpu.make_async_remote_copy(
            src_ref=kv_ref.at[peer // 2], dst_ref=kv_out.at[me], send_sem=send_sem.at[off], recv_sem=recv_sem.at[off],
            device_id={"group": peer}, device_id_type=pl.DeviceIdType.MESH))
        copies[-1].start()
    for off in range(1, chips):
        other = lax.rem(chip + off, chips)
        copies.append(pltpu.make_async_remote_copy(
            src_ref=q_ref.at[other], dst_ref=q_out.at[chip], send_sem=send_sem.at[group + off], recv_sem=recv_sem.at[group + off],
            device_id={"group": 2 * other + core}, device_id_type=pl.DeviceIdType.MESH))
        copies[-1].start()
    for copy in own:
        copy.wait()
    for copy in copies:
        copy.wait()


def spread(q_t, kv_t, collective_id):
    chips = q_t.shape[0]
    sems = 3 * chips
    return pl.pallas_call(
        spread_kernel,
        in_specs=[pl.BlockSpec(memory_space=pltpu.VMEM)] * 2,
        out_specs=[pl.BlockSpec(memory_space=pltpu.VMEM)] * 2,
        out_shape=[jax.ShapeDtypeStruct(q_t.shape, q_t.dtype), jax.ShapeDtypeStruct((2 * chips,) + kv_t.shape[1:], kv_t.dtype)],
        scratch_shapes=[pltpu.SemaphoreType.DMA((sems,)), pltpu.SemaphoreType.DMA((sems,)), pltpu.SemaphoreType.DMA((2,))],
        compiler_params=pltpu.CompilerParams(collective_id=collective_id, has_side_effects=True, vmem_limit_bytes=VMEM_LIMIT),
        name="spread",
    )(q_t, kv_t)


def solution(mesh):
    group_size = mesh.shape["group"]
    chips = group_size // 2
    swap = [(dev, dev ^ 1) for dev in range(group_size)]

    def device_step(x_own, hint_own, in_qkv, in_proj, in_up, in_down, in_norm, out_qkv, out_proj, out_up, out_down, out_norm, zero_proj, hint_proj, skip_proj, final_norm, w_out):
        layers = skip_proj.shape[0]
        tok_own, width = x_own.shape
        heads = in_proj.shape[2]
        head_dim = width // heads
        me = lax.axis_index("group")
        is_base = me % 2 == 0
        branch = jnp.reshape((me % 2).astype(jnp.int32), (1,))
        zero = jnp.zeros((1,), jnp.int32)
        in_proj = in_proj.reshape(in_proj.shape[:2] + (width, width))
        out_proj = out_proj.reshape((1, layers, width, width))
        out_qkv, out_up, out_down, out_norm = out_qkv[None], out_up[None], out_down[None], out_norm[None]

        both = jnp.concatenate([x_own, hint_own], axis=0)
        both_other = lax.ppermute(both, "group", swap)
        x_other, hint_other = both_other[:tok_own], both_other[tok_own:]
        x_local = jnp.where(is_base, jnp.concatenate([x_own, x_other], axis=0), jnp.concatenate([x_other, x_own], axis=0))
        hint_local = jnp.where(is_base, jnp.zeros((2 * tok_own, width), BF16), jnp.concatenate([hint_other, hint_own], axis=0))
        state = (x_local.astype(F32) + mat_f32(hint_local, hint_proj)).astype(BF16)
        sums = []
        for layer in range(layers + 1):
            qkv_t = qkv_call(branch, layer, state, in_norm, in_qkv, heads)
            moved = plane_exchange(qkv_t, 0)
            att_t = attn_call(moved[:, 0], moved[:, 1:])
            back = plane_exchange(att_t, 1).reshape(width, 2 * tok_own)
            state = post_call(branch, layer, back, state, in_norm, in_proj, in_up, in_down)
            ctrl_res = mat_f32(state, zero_proj[layer]).astype(BF16)
            give = jnp.where(is_base, state[tok_own:], ctrl_res[:tok_own])
            keep = jnp.where(is_base, state[:tok_own], ctrl_res[tok_own:])
            got = lax.ppermute(give, "group", swap)
            sums.append((keep.astype(F32) + got.astype(F32)).astype(BF16))
        out_state = sums.pop()
        for layer in range(layers):
            skip_val = sums[layers - 1 - layer]
            merged = (mat_f32(out_state, skip_proj[layer, :width]) + mat_f32(skip_val, skip_proj[layer, width:])).astype(BF16)
            qkv_t = qkv_call(zero, layer, merged, out_norm, out_qkv, heads)
            q_moved, kv_moved = spread(qkv_t[:, 0], qkv_t[:, 1:], 2)
            att_t = attn_call(q_moved, kv_moved)
            back = plane_exchange(att_t, 3).reshape(width, tok_own)
            out_state = post_call(zero, layer, back, merged, out_norm, out_proj, out_up, out_down)
        normed = layer_norm(out_state, final_norm[0], final_norm[1])
        return mat_f32(normed, w_out).astype(BF16)

    tok_spec = P(("data", "group"), None)
    return jax.shard_map(device_step, mesh=mesh, in_specs=(tok_spec, tok_spec) + (P(),) * 15, out_specs=tok_spec, check_vma=False)
```

time: 2600 us -> 627 us (0.24)
  waiting for transfers between devices: 1750 us -> 1.18 us
  Pallas kernels: 0 us -> 560 us
  matrix products: 397 us -> 25.8 us
  local copies, waits for them, and re-layouts: 286 us -> 20.3 us
  other arithmetic: 101 us -> 5.85 us
  starting transfers between devices: 59.5 us -> 3.56 us
    ppermute x26 -> x4, waiting for transfers between devices: 1750 us -> 1.18 us  [the longest x3 0.94 us: device_step(): got = lax.ppermute(give, 'group', swap)]
    pallas_call x0 -> x25, Pallas kernels: none -> 560 us  [the longest x5 222 us: attn_call(): pl.pallas_call(functools.partial(attn_kernel, scale=head_dim ** (-0.5), c...]
    dot_general x29 -> x9, matrix products: 283 us -> 25.8 us  [mat_f32(): return jnp.dot(left_op, right_op, preferred_element_type=F32)]
    slice x32 -> x6, local copies, waits for them, and re-layouts: 212 us -> 11.1 us  [the longest x3 7.18 us: device_step(): att_t = attn_call(moved[:, 0], moved[:, 1:])]
    sub x5 -> x0, matrix products: 114 us -> none  [transformer_block(): att_probs = jax.nn.softmax(scores, axis=-1).astype(jnp.bfloat16)]
    concatenate x15 -> x1, other arithmetic: 92.9 us -> 2.07 us  [device_step(): both = jnp.concatenate([x_own, hint_own], axis=0)]
    ppermute x26 -> x4, starting transfers between devices: 59.5 us -> 3.56 us  [the longest x1 2.03 us: device_step(): both_other = lax.ppermute(both, 'group', swap)]
    concatenate x5 -> x0, local copies, waits for them, and re-layouts: 40.1 us -> none  [gather_half(): jnp.concatenate([gathered, lax.ppermute(gathered, 'group', partner_perm)]...]
  transfers between devices with their start and end apart: 26 -> 4, of which waited for: 24 -> 2; matrix products, arithmetic and copies ran while one was open for 11% -> 2% of each run, Pallas kernels for 0% -> 15%
where the time goes in v1:
time: 627 us; the launch traced here: 617 us
  Pallas kernels  560 us (89%)
  matrix products  25.8 us (4%)
  local copies, waits for them, and re-layouts  20.3 us (3%)
    pallas_call x5, Pallas kernels, attn_call(): pl.pallas_call(functools.partial(attn_kernel, scale=head_dim ** (-0.5), c...  222 us
    pallas_call x8, Pallas kernels, plane_exchange(): pl.pallas_call(plane_exchange_kernel, in_specs=[pl.BlockSpec(memory_space...  167 us
    pallas_call x5, Pallas kernels, post_call(): pl.pallas_call(post_kernel, grid_spec=grid_spec, out_shape=jax.ShapeDtype...  75.5 us
    pallas_call x2, Pallas kernels, spread(): pl.pallas_call(spread_kernel, in_specs=[pl.BlockSpec(memory_space=pltpu.V...  60.7 us
    pallas_call x5, Pallas kernels, qkv_call(): pl.pallas_call(functools.partial(qkv_kernel, heads=heads, head_dim=head_d...  34.2 us
    dot_general x9, matrix products, mat_f32(): return jnp.dot(left_op, right_op, preferred_element_type=F32)  25.8 us
  transfers between devices with their start and end apart: 4, of which 2 were waited for; matrix products, arithmetic and copies ran while one was open for 2% of the time, Pallas kernels for 15%

profile of v1, /device:TPU:97, one launch (start us, length us, event | category | flops | bytes accessed | tf_op | source)
XLA Modules:
  0.0 616.8 jit_solution(8384209938171984439)
XLA Ops:
  0.0 0.0 copy-start
  0.0 2.1 pad_maximum_fusion.1
  2.1 2.0 collective-permute-start
  4.1 1.4 convert_reduce_fusion.2
  5.5 0.2 collective-permute-done
  5.8 0.0 copy-done
  5.8 3.0 add_convert_fusion.u_ref
  8.8 7.3 %ln_qkv.5.x_ref = bf16[16,3,72,256]{3,2,1,0:T(8,128)(2,1)} custom-call(s32[1]{0:T(128)} %bitcast.br_ref, bf16[256,1152]{1,0:T(8,128)(2,1)} %add_convert_fusion.u_ref, bf16[2,3,4,1152]{3,2,1,0:T(4,128)(2,1)} %norm_ref.11, bf16[2,3,1152,3456]{3,2,1,0:T(8,128)(2,1)} %w_ref.5), custom_call_target="tpu_custom_call" | custom-call | flops 2038431744 | bytes 7962624 | tf_op jit(solution)/shard_map/ln_qkv/pallas_call | solution.py:52
  16.1 36.5 %plane_exchange.8 = bf16[16,3,72,256]{3,2,1,0:T(8,128)(2,1)} custom-call(bf16[16,3,72,256]{3,2,1,0:T(8,128)(2,1)} %ln_qkv.5.x_ref), custom_call_target="tpu_custom_call" | custom-call | tf_op jit(solution)/shard_map/plane_exchange/pallas_call | solution.py:241
  52.6 2.4 slice.102.kv_ref
  54.9 1.9 slice_bitcast_fusion.2.q_ref
  56.9 53.5 %attention.5.x_ref = bf16[16,72,256]{2,1,0:T(8,128)(2,1)} custom-call(bf16[16,72,256]{2,1,0:T(8,128)(2,1)} %slice_bitcast_fusion.2.q_ref, bf16[16,2,72,256]{3,2,1,0:T(8,128)(2,1)} %slice.102.kv_ref), custom_call_target="tpu_custom_call" | custom-call | flops 4831838208 | bytes 4718592 | tf_op jit(solution)/shard_map/attention/pallas_call | solution.py:188
  110.3 12.1 %plane_exchange.9 = bf16[16,72,256]{2,1,0:T(8,128)(2,1)} custom-call(bf16[16,72,256]{2,1,0:T(8,128)(2,1)} %attention.5.x_ref), custom_call_target="tpu_custom_call" | custom-call | tf_op jit(solution)/shard_map/plane_exchange/pallas_call | solution.py:241
  122.5 16.3 %proj_mlp.5.u_ref = bf16[256,1152]{1,0:T(8,128)(2,1)} custom-call(s32[1]{0:T(128)} %bitcast.br_ref, bf16[1152,256]{1,0:T(8,128)(2,1)} %bitcast.84, bf16[256,1152]{1,0:T(8,128)(2,1)} %add_convert_fusion.u_ref, bf16[2,3,4,1152]{3,2,1,0:T(4,128)(2,1)} %norm_ref.11, bf16[2,3,1152,1152]{3,2,1,0:T(8,128)(2,1)} %bitcast.73, bf16[2,3,1152,4608]{3,2,1,0:T(8,128)(2,1)} %w1_ref.5, ...), custom_call_target="tpu_custom_call" | custom-call | flops 6115295232 | bytes 23887872 | tf_op jit(solution)/shard_map/proj_mlp/pallas_call | solution.py:110
  138.8 7.3 %ln_qkv.6.x_ref = bf16[16,3,72,256]{3,2,1,0:T(8,128)(2,1)} custom-call(s32[1]{0:T(128)} %bitcast.br_ref, bf16[256,1152]{1,0:T(8,128)(2,1)} %proj_mlp.5.u_ref, bf16[2,3,4,1152]{3,2,1,0:T(4,128)(2,1)} %norm_ref.11, bf16[2,3,1152,3456]{3,2,1,0:T(8,128)(2,1)} %w_ref.5), custom_call_target="tpu_custom_call" | custom-call | flops 2038431744 | bytes 7962624 | tf_op jit(solution)/shard_map/ln_qkv/pallas_call | solution.py:52
  146.1 35.1 %plane_exchange.10 = bf16[16,3,72,256]{3,2,1,0:T(8,128)(2,1)} custom-call(bf16[16,3,72,256]{3,2,1,0:T(8,128)(2,1)} %ln_qkv.6.x_ref), custom_call_target="tpu_custom_call" | custom-call | tf_op jit(solution)/shard_map/plane_exchange/pallas_call | solution.py:241
  181.1 2.4 slice.104.kv_ref
  183.5 1.9 slice_bitcast_fusion.1.q_ref
  185.4 53.6 %attention.6.x_ref = bf16[16,72,256]{2,1,0:T(8,128)(2,1)} custom-call(bf16[16,72,256]{2,1,0:T(8,128)(2,1)} %slice_bitcast_fusion.1.q_ref, bf16[16,2,72,256]{3,2,1,0:T(8,128)(2,1)} %slice.104.kv_ref), custom_call_target="tpu_custom_call" | custom-call | flops 4831838208 | bytes 4718592 | tf_op jit(solution)/shard_map/attention/pallas_call | solution.py:188
  239.1 14.1 %plane_exchange.11 = bf16[16,72,256]{2,1,0:T(8,128)(2,1)} custom-call(bf16[16,72,256]{2,1,0:T(8,128)(2,1)} %attention.6.x_ref), custom_call_target="tpu_custom_call" | custom-call | tf_op jit(solution)/shard_map/plane_exchange/pallas_call | solution.py:241
  253.2 16.3 %proj_mlp.6.u_ref = bf16[256,1152]{1,0:T(8,128)(2,1)} custom-call(s32[1]{0:T(128)} %bitcast.br_ref, bf16[1152,256]{1,0:T(8,128)(2,1)} %bitcast.86, bf16[256,1152]{1,0:T(8,128)(2,1)} %proj_mlp.5.u_ref, bf16[2,3,4,1152]{3,2,1,0:T(4,128)(2,1)} %norm_ref.11, bf16[2,3,1152,1152]{3,2,1,0:T(8,128)(2,1)} %bitcast.74, bf16[2,3,1152,4608]{3,2,1,0:T(8,128)(2,1)} %w1_ref.5, ...), custom_call_target="tpu_custom_call" | custom-call | flops 6115295232 | bytes 23887872 | tf_op jit(solution)/shard_map/proj_mlp/pallas_call | solution.py:110
  269.5 7.3 %ln_qkv.7.x_ref = bf16[16,3,72,256]{3,2,1,0:T(8,128)(2,1)} custom-call(s32[1]{0:T(128)} %bitcast.br_ref, bf16[256,1152]{1,0:T(8,128)(2,1)} %proj_mlp.6.u_ref, bf16[2,3,4,1152]{3,2,1,0:T(4,128)(2,1)} %norm_ref.11, bf16[2,3,1152,3456]{3,2,1,0:T(8,128)(2,1)} %w_ref.5), custom_call_target="tpu_custom_call" | custom-call | flops 2038431744 | bytes 7962624 | tf_op jit(solution)/shard_map/ln_qkv/pallas_call | solution.py:52
  276.8 32.4 %plane_exchange.12 = bf16[16,3,72,256]{3,2,1,0:T(8,128)(2,1)} custom-call(bf16[16,3,72,256]{3,2,1,0:T(8,128)(2,1)} %ln_qkv.7.x_ref), custom_call_target="tpu_custom_call" | custom-call | tf_op jit(solution)/shard_map/plane_exchange/pallas_call | solution.py:241
  309.3 0.0 copy-start.3
  309.3 2.4 slice.106.kv_ref
  311.7 1.9 slice_bitcast_fusion.q_ref
  313.6 0.0 copy-done.3
  313.6 2.8 fusion.24
  316.4 0.0 copy-done.2
  316.4 2.7 fusion.27
  319.2 53.7 %attention.7.x_ref = bf16[16,72,256]{2,1,0:T(8,128)(2,1)} custom-call(bf16[16,72,256]{2,1,0:T(8,128)(2,1)} %slice_bitcast_fusion.q_ref, bf16[16,2,72,256]{3,2,1,0:T(8,128)(2,1)} %slice.106.kv_ref), custom_call_target="tpu_custom_call" | custom-call | flops 4831838208 | bytes 4718592 | tf_op jit(solution)/shard_map/attention/pallas_call | solution.py:188
  372.9 16.9 %plane_exchange.13 = bf16[16,72,256]{2,1,0:T(8,128)(2,1)} custom-call(bf16[16,72,256]{2,1,0:T(8,128)(2,1)} %attention.7.x_ref), custom_call_target="tpu_custom_call" | custom-call | tf_op jit(solution)/shard_map/plane_exchange/pallas_call | solution.py:241
  389.8 16.3 %proj_mlp.7 = bf16[256,1152]{1,0:T(8,128)(2,1)} custom-call(s32[1]{0:T(128)} %bitcast.br_ref, bf16[1152,256]{1,0:T(8,128)(2,1)} %bitcast.85, bf16[256,1152]{1,0:T(8,128)(2,1)} %proj_mlp.6.u_ref, bf16[2,3,4,1152]{3,2,1,0:T(4,128)(2,1)} %norm_ref.11, bf16[2,3,1152,1152]{3,2,1,0:T(8,128)(2,1)} %bitcast.75, bf16[2,3,1152,4608]{3,2,1,0:T(8,128)(2,1)} %w1_ref.5, ...), custom_call_target="tpu_custom_call" | custom-call | flops 6115295232 | bytes 23887872 | tf_op jit(solution)/shard_map/proj_mlp/pallas_call | solution.py:110
  406.1 3.0 fusion.21
  409.2 0.8 collective-permute-start.1
  410.1 0.1 collective-permute-start.2
  410.2 0.6 collective-permute-start.3
  410.8 0.9 collective-permute-done.2
  411.7 2.3 fusion.6
  414.1 0.0 collective-permute-done.1
  414.1 3.1 fusion.39.u_ref
  417.2 6.2 %ln_qkv.8 = bf16[16,3,72,128]{3,2,1,0:T(8,128)(2,1)} custom-call(s32[1]{0:T(128)} %constant.23.clone.1.br_ref, bf16[128,1152]{1,0:T(8,128)(2,1)} %fusion.39.u_ref, bf16[1,2,4,1152]{3,2,1,0:T(4,128)(2,1)} %bitcast.89, bf16[1,2,1152,3456]{3,2,1,0:T(8,128)(2,1)} %bitcast.80), custom_call_target="tpu_custom_call" | custom-call | flops 1019215872 | bytes 7962624 | tf_op jit(solution)/shard_map/ln_qkv/pallas_call | solution.py:52
  423.4 2.0 slice.143.kv_ref
  425.4 1.7 slice_bitcast_fusion.4.q_ref
  427.0 29.6 %spread.2 = (bf16[16,72,128]{2,1,0:T(8,128)(2,1)}, bf16[32,2,72,128]{3,2,1,0:T(8,128)(2,1)}) custom-call(bf16[16,72,128]{2,1,0:T(8,128)(2,1)} %slice_bitcast_fusion.4.q_ref, bf16[16,2,72,128]{3,2,1,0:T(8,128)(2,1)} %slice.143.kv_ref), custom_call_target="tpu_custom_call" | custom-call | tf_op jit(solution)/shard_map/spread/pallas_call | solution.py:286
  456.7 31.0 %attention.8.x_ref = bf16[16,72,128]{2,1,0:T(8,128)(2,1)} custom-call(bf16[16,72,128]{2,1,0:T(8,128)(2,1)} %get-tuple-element.9.q_ref, bf16[32,2,72,128]{3,2,1,0:T(8,128)(2,1)} %get-tuple-element.10.kv_ref), custom_call_target="tpu_custom_call" | custom-call | flops 2415919104 | bytes 4718592 | tf_op jit(solution)/shard_map/attention/pallas_call | solution.py:188
  487.7 9.7 %plane_exchange.14 = bf16[16,72,128]{2,1,0:T(8,128)(2,1)} custom-call(bf16[16,72,128]{2,1,0:T(8,128)(2,1)} %attention.8.x_ref), custom_call_target="tpu_custom_call" | custom-call | tf_op jit(solution)/shard_map/plane_exchange/pallas_call | solution.py:241
  497.4 13.2 %proj_mlp.8 = bf16[128,1152]{1,0:T(8,128)(2,1)} custom-call(s32[1]{0:T(128)} %constant.23.clone.1.br_ref, bf16[1152,128]{1,0:T(8,128)(2,1)} %bitcast.88, bf16[128,1152]{1,0:T(8,128)(2,1)} %fusion.39.u_ref, bf16[1,2,4,1152]{3,2,1,0:T(4,128)(2,1)} %bitcast.90, bf16[1,2,1152,1152]{3,2,1,0:T(8,128)(2,1)} %bitcast.82, bf16[1,2,1152,4608]{3,2,1,0:T(8,128)(2,1)} %bitcast.76, ...), custom_call_target="tpu_custom_call" | custom-call | flops 3057647616 | bytes 23887872 | tf_op jit(solution)/shard_map/proj_mlp/pallas_call | solution.py:110
  510.7 2.4 fusion.4
  513.1 0.0 collective-permute-done.3
  513.1 3.1 fusion.36.u_ref
  516.2 6.2 %ln_qkv.9 = bf16[16,3,72,128]{3,2,1,0:T(8,128)(2,1)} custom-call(s32[1]{0:T(128)} %constant.23.clone.1.br_ref, bf16[128,1152]{1,0:T(8,128)(2,1)} %fusion.36.u_ref, bf16[1,2,4,1152]{3,2,1,0:T(4,128)(2,1)} %bitcast.91, bf16[1,2,1152,3456]{3,2,1,0:T(8,128)(2,1)} %bitcast.81), custom_call_target="tpu_custom_call" | custom-call | flops 1019215872 | bytes 7962624 | tf_op jit(solution)/shard_map/ln_qkv/pallas_call | solution.py:52
  522.4 2.0 slice.149.kv_ref
  524.3 1.7 slice_bitcast_fusion.3.q_ref
  526.0 31.1 %spread.3 = (bf16[16,72,128]{2,1,0:T(8,128)(2,1)}, bf16[32,2,72,128]{3,2,1,0:T(8,128)(2,1)}) custom-call(bf16[16,72,128]{2,1,0:T(8,128)(2,1)} %slice_bitcast_fusion.3.q_ref, bf16[16,2,72,128]{3,2,1,0:T(8,128)(2,1)} %slice.149.kv_ref), custom_call_target="tpu_custom_call" | custom-call | tf_op jit(solution)/shard_map/spread/pallas_call | solution.py:286
  557.1 30.6 %attention.9.x_ref = bf16[16,72,128]{2,1,0:T(8,128)(2,1)} custom-call(bf16[16,72,128]{2,1,0:T(8,128)(2,1)} %get-tuple-element.11.q_ref, bf16[32,2,72,128]{3,2,1,0:T(8,128)(2,1)} %get-tuple-element.12.kv_ref), custom_call_target="tpu_custom_call" | custom-call | flops 2415919104 | bytes 4718592 | tf_op jit(solution)/shard_map/attention/pallas_call | solution.py:188
  587.7 10.0 %plane_exchange.15 = bf16[16,72,128]{2,1,0:T(8,128)(2,1)} custom-call(bf16[16,72,128]{2,1,0:T(8,128)(2,1)} %attention.9.x_ref), custom_call_target="tpu_custom_call" | custom-call | tf_op jit(solution)/shard_map/plane_exchange/pallas_call | solution.py:241
  597.8 0.0 copy-start.6
  597.8 0.0 copy-start.7
  597.8 0.0 copy-start.1
  597.8 13.3 %proj_mlp.9 = bf16[128,1152]{1,0:T(8,128)(2,1)} custom-call(s32[1]{0:T(128)} %constant.23.clone.1.br_ref, bf16[1152,128]{1,0:T(8,128)(2,1)} %bitcast.87, bf16[128,1152]{1,0:T(8,128)(2,1)} %fusion.36.u_ref, bf16[1,2,4,1152]{3,2,1,0:T(4,128)(2,1)} %bitcast.92, bf16[1,2,1152,1152]{3,2,1,0:T(8,128)(2,1)} %bitcast.83, bf16[1,2,1152,4608]{3,2,1,0:T(8,128)(2,1)} %bitcast.77, ...), custom_call_target="tpu_custom_call" | custom-call | flops 3057647616 | bytes 23887872 | tf_op jit(solution)/shard_map/proj_mlp/pallas_call | solution.py:110
  611.2 1.1 convert_reduce_fusion
  612.3 1.2 fusion.50
  613.5 3.2 convolution_convert_fusion
  (14 shorter events, 0.2 us)
Async XLA Ops:
  0.0 5.8 copy-start
  2.1 3.7 collective-permute-start
  309.3 4.4 copy-start.3
  313.6 2.8 copy-start.2
  406.1 3.0 copy-start.5
  406.1 3.9 copy-start.4
  409.2 4.9 collective-permute-start.1
  410.1 1.7 collective-permute-start.2
  410.2 102.9 %collective-permute-start.3 = (bf16[128,1152]{1,0:T(8,128)(2,1)S(1)}, bf16[128,1152]{1,0:T(8,128)(2,1)S(1)}, u32[]{:S(2)}, u32[]{:S(2)}) collective-permute-start(bf16[128,1152]{1,0:T(8,128)(2,1)S(1)} %slice_select_fusion), channel_id=1, source_target_pairs={{0,1},{1,0},{2,3},{3,2},{4,5},{5,4},{6,7},{7,6},{8,9},{9,8},{10,11... | collective-permute-start | bytes 884744 | tf_op jit(solution)/shard_map/ppermute | solution.py:331
  597.8 15.7 %copy-start.6 = (f32[1152]{0:T(1024)S(1)}, f32[1152]{0:T(1024)}, u32[]{:S(2)}) copy-start(f32[1152]{0:T(1024)} %get-tuple-element.13) | copy-start | bytes 13828
  597.8 15.7 %copy-start.7 = (f32[1152]{0:T(1024)S(1)}, f32[1152]{0:T(1024)}, u32[]{:S(2)}) copy-start(f32[1152]{0:T(1024)} %get-tuple-element.14) | copy-start | bytes 13828
  597.8 18.9 %copy-start.1 = (bf16[1152,1152]{1,0:T(8,128)(2,1)S(1)}, bf16[1152,1152]{1,0:T(8,128)(2,1)}, u32[]{:S(2)}) copy-start(bf16[1152,1152]{1,0:T(8,128)(2,1)} %param.30) | copy-start | bytes 7962628
